TPU v7x, 32 devices: a whole 2x2x4 slice. The times are simulated.
32 devices in a mesh: dp: 8 (over y, x, core), head: 4 (over z).
Axes of the slice: x: 2, y: 2, z: 4, core: 2. Of those that a mesh axis runs over, the one named last changes fastest.
Arguments:
- feats: bfloat16 [4, 4096, 384], P('head', 'dp'), may hold values from -6 to 6
- valid: int32 [16], P('dp'), may hold values from 1 to 256
- owner_map: int32 [16], P('dp'), may hold values from 0 to 7, as said below
- w_conv: bfloat16 [4, 3, 384, 384], P('head', None, 'dp'), may hold values from -0.11785113 to 0.11785113
- w_mid: bfloat16 [4, 384, 384], P('head', 'dp'), may hold values from -0.20412415 to 0.20412415
- w_out: bfloat16 [4, 384], P('head', 'dp'), may hold values from -0.20412415 to 0.20412415
Outputs:
- grad_feats: bfloat16 [4, 8192, 384], P('head', 'dp')
- grad_conv: float32 [4, 3, 384, 384], P('head', None, 'dp')
- grad_mid: float32 [4, 384, 384], P('head', 'dp')
- grad_out: float32 [4, 384], P('head', 'dp')
Inputs may be any that keep to these rules, and one draw needn't show every extreme that they name: `owner_map`: image o is held by index o of dp. Every image owns 1 to 4 blocks; a quarter of the images own exactly 4. The 2 blocks of one index of dp belong to 2 different images.
All inputs are finite; a program needn't handle non-finite values.
Results may differ from a plain program's by a relative error of at most 0.019.
Values may be sent and summed in bfloat16 or wider, within the bound.
A program may use at most 128 MiB of HBM per device.

v0:
```python
import jax
import jax.numpy as jnp
from jax import lax
from jax.sharding import PartitionSpec as P

D = 384
TAPS = 4
BT = 256


def entering(shard, axis, combine, identity):
    count, index = (lax.axis_size(axis), lax.axis_index(axis))
    everything = lax.all_gather(shard, axis)
    start = jnp.broadcast_to(jnp.asarray(identity, shard.dtype), shard.shape)

    def lap(k, before):
        reached = k < index
        new = combine(before, everything[k])
        return jnp.where(reached, new, before)

    return lax.fori_loop(0, count, lap, start)


def activate(value):
    return 0.2 * value + 0.8 * jax.nn.softplus(value)


def derivative(value):
    return 0.2 + 0.8 * jax.nn.sigmoid(value)


def flatten(array):
    return array.reshape(-1, array.shape[-1])


def add_counts(earlier, later):
    return earlier + later


def forward_pass(blocks, mask, conv_w, mid_w, out_w):
    count = blocks.shape[0]
    width = blocks.shape[2]
    masked = (blocks * mask[:, :, None]).astype(jnp.bfloat16)
    zero_row = jnp.zeros((count, 1, width), jnp.bfloat16)
    previous = jnp.concatenate([zero_row, masked[:, :-1]], 1)
    following = jnp.concatenate([masked[:, 1:], zero_row], 1)
    first_pre = jnp.dot(flatten(previous), conv_w[0], preferred_element_type=jnp.float32)
    first_pre = first_pre + jnp.dot(flatten(masked), conv_w[1], preferred_element_type=jnp.float32)
    first_pre = first_pre + jnp.dot(
        flatten(following), conv_w[2], preferred_element_type=jnp.float32
    )
    first_act = activate(first_pre)
    first_low = first_act.astype(jnp.bfloat16)
    second_pre = jnp.dot(first_low, mid_w, preferred_element_type=jnp.float32)
    second_act = activate(second_pre) + first_act
    logits = jnp.dot(second_act, out_w.astype(jnp.float32), precision=lax.Precision.HIGHEST)
    return ((previous, masked, following, first_pre, first_low, second_pre, second_act), logits)


def backward_pass(saved, upstream, mask, conv_w, mid_w, out_w):
    previous, masked, following, first_pre, first_low, second_pre, second_act = saved
    count, length, width = masked.shape
    grad_second = upstream[:, None] * out_w.astype(jnp.float32)[None, :]
    grad_mid_pre = (grad_second * derivative(second_pre)).astype(jnp.bfloat16)
    grad_first = jnp.dot(grad_mid_pre, mid_w.T, preferred_element_type=jnp.float32) + grad_second
    grad_first_pre = (grad_first * derivative(first_pre)).astype(jnp.bfloat16)

    def through(index):
        return jnp.dot(grad_first_pre, conv_w[index].T, preferred_element_type=jnp.float32).reshape(
            count, length, width
        )

    zero_row = jnp.zeros((count, 1, width), jnp.float32)
    from_next = through(0)
    from_prev = through(2)
    total = (
        through(1)
        + jnp.concatenate([from_next[:, 1:], zero_row], 1)
        + jnp.concatenate([zero_row, from_prev[:, :-1]], 1)
    )
    grad_input = (total * mask[:, :, None]).astype(jnp.bfloat16)
    grad_conv = jnp.stack(
        [
            jnp.dot(flatten(previous).T, grad_first_pre, preferred_element_type=jnp.float32),
            jnp.dot(flatten(masked).T, grad_first_pre, preferred_element_type=jnp.float32),
            jnp.dot(flatten(following).T, grad_first_pre, preferred_element_type=jnp.float32),
        ]
    )
    grad_mid = jnp.dot(first_low.T, grad_mid_pre, preferred_element_type=jnp.float32)
    grad_out = jnp.dot(upstream, second_act, precision=lax.Precision.HIGHEST)
    return (grad_input, grad_conv, grad_mid, grad_out)


def pack_blocks(picks, blocks):
    packed = jnp.dot(
        picks.astype(jnp.bfloat16),
        flatten(blocks.reshape(blocks.shape[0], -1)),
        preferred_element_type=jnp.float32,
    )
    return packed.astype(jnp.bfloat16).reshape(-1, 1, blocks.shape[1], blocks.shape[2])


def place_blocks(received, codes, capacity):
    entries = codes[..., 0].astype(jnp.float32).reshape(-1)
    table = (entries[None, :] - 1.0 == jnp.arange(capacity, dtype=jnp.float32)[:, None]).astype(
        jnp.float32
    )
    rows_flat = received.reshape(entries.shape[0], -1)
    placed = jnp.dot(
        table.astype(jnp.bfloat16), rows_flat, preferred_element_type=jnp.float32
    ).astype(jnp.bfloat16)
    return (placed.reshape(capacity, received.shape[2], received.shape[3]), table)


def per_device(feats, valid, owner_map, w_conv, w_mid, w_out):
    conv_all, mid_all, out_all = (
        lax.all_gather(w_conv, "dp", axis=2, tiled=True),
        lax.all_gather(w_mid, "dp", axis=1, tiled=True),
        lax.all_gather(w_out, "dp", axis=1, tiled=True),
    )
    conv_w = conv_all[0]
    mid_w = mid_all[0]
    out_w = out_all[0]
    devices = lax.axis_size("dp")
    capacity = devices // 2
    local = owner_map.shape[0]
    owners = jnp.arange(devices, dtype=jnp.int32)
    member_int = (owner_map[:, None] == owners[None, :]).astype(jnp.int32)
    earlier = jnp.cumsum(member_int, 0) - member_int
    within = jnp.sum(earlier * member_int, 1)
    lower = entering(jnp.sum(member_int, 0), "dp", add_counts, jnp.zeros((devices,), jnp.int32))
    slots = jnp.sum(member_int * lower[None, :], 1) + within
    tokens = lax.psum(jnp.sum(member_int * valid[:, None], 0).astype(jnp.float32), "dp")
    scale_norm = jnp.sqrt(TAPS * tokens)
    picks = (owner_map[None, :] == owners[:, None]).astype(jnp.float32)
    labels = jnp.stack([slots + 1, valid], 1).astype(jnp.float32)
    meta = (
        jnp.dot(picks, labels, precision=lax.Precision.HIGHEST)
        .astype(jnp.bfloat16)
        .reshape(devices, 1, 2)
    )
    blocks_here = feats[0].reshape(local, BT, D)
    slot_valid = valid.astype(jnp.float32)
    members = member_int.astype(jnp.float32)
    count = blocks_here.shape[0]
    mask = (jnp.arange(BT, dtype=jnp.float32)[None, :] < slot_valid[:, None]).astype(jnp.float32)
    saved, logits = forward_pass(blocks_here, mask, conv_w, mid_w, out_w)
    block_sums = jnp.sum(logits.reshape(count, BT) * mask, 1)
    totals = lax.psum(jnp.dot(block_sums, members, precision=lax.Precision.HIGHEST), ("dp", "head"))
    strength = totals / scale_norm
    factor = -BT * jax.nn.sigmoid(-strength) / scale_norm
    upstream = (jnp.dot(members, factor, precision=lax.Precision.HIGHEST)[:, None] * mask).reshape(
        -1
    )
    grad_input, grad_conv, grad_mid, grad_out = backward_pass(
        saved, upstream, mask, conv_w, mid_w, out_w
    )
    outgoing_grads = pack_blocks(picks, grad_input)
    back, back_meta = (
        lax.all_to_all(outgoing_grads, "dp", split_axis=0, concat_axis=0, tiled=True),
        lax.all_to_all(meta, "dp", split_axis=0, concat_axis=0, tiled=True),
    )
    placed, ignored = place_blocks(back, back_meta, capacity)
    returned = placed.reshape(1, capacity * BT, D)
    conv_part, mid_part, out_part = (
        lax.psum_scatter(
            grad_conv.astype(jnp.bfloat16), "dp", scatter_dimension=1, tiled=True
        ).astype(jnp.float32),
        lax.psum_scatter(
            grad_mid.astype(jnp.bfloat16), "dp", scatter_dimension=0, tiled=True
        ).astype(jnp.float32),
        lax.psum_scatter(
            grad_out.astype(jnp.bfloat16), "dp", scatter_dimension=0, tiled=True
        ).astype(jnp.float32),
    )
    total_blocks = devices * local
    return (
        returned,
        (conv_part / total_blocks)[None],
        (mid_part / total_blocks)[None],
        (out_part / total_blocks)[None],
    )


def solution(mesh):
    in_specs = (
        P("head", "dp", None),
        P("dp"),
        P("dp"),
        P("head", None, "dp", None),
        P("head", "dp", None),
        P("head", "dp"),
    )
    out_specs = (
        P("head", "dp", None),
        P("head", None, "dp", None),
        P("head", "dp", None),
        P("head", "dp"),
    )
    return jax.shard_map(
        per_device, mesh=mesh, in_specs=in_specs, out_specs=out_specs, check_vma=False
    )
```

profile of v0, /device:TPU:0, one launch (start us, length us, event | category | flops | bytes accessed | tf_op | source)
XLA Modules:
  0.0 207.6 jit_solution(6444904071127117235)
XLA Ops:
  8.7 1.3 fusion.81
  10.9 9.5 %all-reduce.4 = s32[64]{0:T(128)S(1)} all-reduce(s32[64]{0:T(128)S(1)} %dynamic-update-slice), channel_id=2, replica_groups=mesh['dp'=8,'head'=4] {'dp'}, use_global_device_ids=true, to_apply=%add.4 | all-reduce | flops 64 | bytes 512
  20.8 0.9 select_reduce_fusion.1
  21.7 0.8 fusion.9
  23.2 3.3 %all-to-all-start = ((bf16[8,1,2]{2,1,0:T(2,128)(2,1)}), bf16[8,1,2]{2,1,0:T(2,128)(2,1)S(1)}, u32[]{:S(2)}, u32[]{:S(2)}) async-start(bf16[8,1,2]{2,1,0:T(2,128)(2,1)} %copy.14), calls=%async_computation | async-start | bytes 8192 | tf_op jit(solution)/shard_map/all_to_all | solution.py:161
  27.9 0.9 dynamic-update-slice.1
  28.7 14.3 %all-reduce.5 = bf16[384]{0:T(512)(128)(2,1)S(1)} all-reduce(bf16[384]{0:T(512)(128)(2,1)S(1)} %dynamic-update-slice.1), channel_id=1, replica_groups=mesh['dp'=8,'head'=4] {'dp'}, use_global_device_ids=true, to_apply=%add.5 | all-reduce | flops 384 | bytes 1536 | tf_op jit(solution)/shard_map/squeeze | solution.py:123
  43.1 11.8 %psum.15 = f32[8]{0:T(128)S(1)} all-reduce(f32[8]{0:T(128)S(1)} %convert_element_type.137), channel_id=1, replica_groups=mesh['dp'=8,'head'=4] {'dp'}, use_global_device_ids=true, to_apply=%region_9.10 | all-reduce | flops 8 | bytes 64 | tf_op jit(solution)/shard_map/psum | solution.py:133
  54.9 8.6 %all_gather.18 = bf16[1,384,384]{2,1,0:T(8,128)(2,1)S(1)} all-gather(bf16[1,48,384]{2,1,0:T(8,128)(2,1)} %param.12), channel_id=1, replica_groups=mesh['dp'=8,'head'=4] {'dp'}, dimensions={1}, use_global_device_ids=true | all-gather | bytes 331776 | tf_op jit(solution)/shard_map/all_gather | solution.py:118
  63.6 1.1 multiply_convert_fusion.1
  65.6 10.7 %all_gather.17 = bf16[1,3,384,384]{3,2,1,0:T(8,128)(2,1)S(1)} all-gather(bf16[1,3,48,384]{3,2,1,0:T(8,128)(2,1)S(1)} %copy-done.2), channel_id=1, replica_groups=mesh['dp'=8,'head'=4] {'dp'}, dimensions={2}, use_global_device_ids=true | all-gather | bytes 995328 | tf_op jit(solution)/shard_map/all_gather | solution.py:117
  77.6 2.4 %fusion.15 = (f32[512,384]{1,0:T(8,128)S(1)}, f32[512,384]{1,0:T(8,128)}) fusion(f32[512,384]{1,0:T(8,128)S(1)} %convolution_add_fusion.2, bf16[1,384,384]{2,1,0:T(8,128)(2,1)S(1)} %all_gather.18), kind=kOutput, calls=%fused_computation.35 | convolution fusion | flops 156696576 | bytes 2654208 | tf_op jit(solution)/shard_map/dot_general | solution.py:54
  80.9 39.5 %psum.14 = f32[8]{0:T(128)S(1)} all-reduce(f32[8]{0:T(128)S(1)} %convolution_bitcast_fusion.1), channel_id=1, replica_groups=mesh['dp'=8,'head'=4] {'dp','head'}, use_global_device_ids=true, to_apply=%region_7.8 | all-reduce | flops 8 | bytes 64 | tf_op jit(solution)/shard_map/psum | solution.py:149
  120.7 3.1 %convolution_convert_fusion.2 = bf16[384,384]{1,0:T(8,128)(2,1)} fusion(f32[512,384]{1,0:T(8,128)} %copy-done.1, f32[512,384]{1,0:T(8,128)} %get-tuple-element.119, f32[384]{0:T(512)S(1)} %mul.122, f32[512]{0:T(512)S(1)} %bitcast.129), kind=kOutput, calls=%fused_computation.15 | convolution fusion | flops 154681344 | bytes 1871360 | tf_op jit(solution)/shard_map/dot_general | solution.py:89
  123.8 2.0 fusion.4
  127.1 1.0 pad_maximum_fusion
  130.5 1.4 copy.15
  131.8 4.0 %all-to-all-start.1 = ((bf16[8,1,256,384]{3,2,1,0:T(8,128)(2,1)}), bf16[8,1,256,384]{3,2,1,0:T(8,128)(2,1)S(1)}, u32[]{:S(2)}, u32[]{:S(2)}) async-start(bf16[8,1,256,384]{3,2,1,0:T(8,128)(2,1)} %copy.15), calls=%async_computation.1 | async-start | bytes 3145728 | tf_op jit(solution)/shard_map/all_to_all | solution.py:160
  136.9 27.6 %all-reduce.6 = bf16[384]{0:T(512)(128)(2,1)S(1)} all-reduce(bf16[384]{0:T(512)(128)(2,1)S(1)} %convolution_reduce_fusion), channel_id=5, replica_groups=mesh['dp'=8,'head'=4] {'dp'}, use_global_device_ids=true, to_apply=%region_12.13.clone | all-reduce | flops 384 | bytes 1536
  165.2 1.4 multiply_bitcast_fusion.1
  166.6 29.6 %reduce-scatter.3.cloned.1.call-done = bf16[3,48,384]{2,1,0:T(8,128)(2,1)} async-done(((bf16[3,384,384]{2,1,0:T(8,128)(2,1)}), bf16[3,48,384]{2,1,0:T(8,128)(2,1)}) %reduce-scatter.3.cloned.1.call-update) | async-done | bytes 110608 | tf_op jit(solution)/shard_map/reduce_scatter | solution.py:166
  196.3 1.6 multiply_bitcast_fusion
  197.9 0.9 copy.20
  199.4 1.4 reshape_reshape.3
  (71 shorter events, 12.4 us)
Async XLA Ops:
  23.2 108.6 %all-to-all-start = ((bf16[8,1,2]{2,1,0:T(2,128)(2,1)}), bf16[8,1,2]{2,1,0:T(2,128)(2,1)S(1)}, u32[]{:S(2)}, u32[]{:S(2)}) async-start(bf16[8,1,2]{2,1,0:T(2,128)(2,1)} %copy.14), calls=%async_computation | async-start | bytes 8192 | tf_op jit(solution)/shard_map/all_to_all | solution.py:161
  26.5 138.7 %reduce-scatter.5.cloned.1.call-start = ((), (), s32[]{:S(2)}) async-start(), calls=%async_computation.5 | async-start | bytes 331776 | tf_op jit(solution)/shard_map/reduce_scatter | solution.py:169
  64.7 0.9 copy-start.2
  64.9 11.8 %copy-start = (bf16[1,512,384]{2,1,0:T(8,128)(2,1)S(1)}, bf16[1,512,384]{2,1,0:T(8,128)(2,1)}, u32[]{:S(2)}) copy-start(bf16[1,512,384]{2,1,0:T(8,128)(2,1)} %param.8) | copy-start | bytes 1179652
  77.6 2.4 %copy-start.1 = (f32[512,384]{1,0:T(8,128)}, f32[512,384]{1,0:T(8,128)S(1)}, u32[]{:S(2)}) copy-start(f32[512,384]{1,0:T(8,128)S(1)} %convolution_add_fusion.2) | copy-start | bytes 2359300
  77.6 3.1 %copy-start.3 = (s32[2]{0:T(128)S(1)}, s32[2]{0:T(128)}, u32[]{:S(2)}) copy-start(s32[2]{0:T(128)} %param.10) | copy-start | bytes 28
  80.9 42.9 %copy-start.5 = (f32[384]{0:T(512)}, f32[384]{0:T(512)S(1)}, u32[]{:S(2)}) copy-start(f32[384]{0:T(512)S(1)} %mul.122) | copy-start | bytes 4612
  120.7 3.1 %copy-start.6 = (f32[1,2,2,128]{3,1,2,0:T(2,128)}, f32[1,2,2,128]{3,1,2,0:T(2,128)S(1)}, u32[]{:S(2)}) copy-start(f32[1,2,2,128]{3,1,2,0:T(2,128)S(1)} %copy.18) | copy-start | bytes 6148
  123.8 72.5 %reduce-scatter.3.cloned.1.call-start = ((), (), s32[]{:S(2)}) async-start(), calls=%async_computation.4 | async-start | bytes 995328 | tf_op jit(solution)/shard_map/reduce_scatter | solution.py:166
  129.0 0.9 copy-start.4
  131.8 66.1 %all-to-all-start.1 = ((bf16[8,1,256,384]{3,2,1,0:T(8,128)(2,1)}), bf16[8,1,256,384]{3,2,1,0:T(8,128)(2,1)S(1)}, u32[]{:S(2)}, u32[]{:S(2)}) async-start(bf16[8,1,256,384]{3,2,1,0:T(8,128)(2,1)} %copy.15), calls=%async_computation.1 | async-start | bytes 3145728 | tf_op jit(solution)/shard_map/all_to_all | solution.py:160
Sparse Core Ops, SparseCore 0:
  123.9 35.1 reduce-scatter.4
  162.4 33.8 reduce-scatter.2
where the time goes:
time: 208 us
  blocking collectives  122 us (59%)
  waiting for transfers between devices  29.7 us (14%)
  between operations  16.3 us (8%)
  matrix products  14.4 us (7%)
  other arithmetic  9.45 us (5%)
  local copies, waits for them, and re-layouts  8.17 us (4%)
  starting transfers between devices  7.35 us (4%)
    psum x1, blocking collectives, per_device(): lax.psum(jnp.dot(block_sums, members, precision=lax.Precision.HIGHEST), (...  39.5 us
    unnamed x2, blocking collectives  37.1 us
    reduce_scatter x1, waiting for transfers between devices, per_device(): lax.psum_scatter(grad_conv.astype(jnp.bfloat16), 'dp', scatter_dimension=...  29.6 us
    squeeze x1, blocking collectives, per_device(): out_w = out_all[0]  14.3 us
    psum x1, blocking collectives, per_device(): lax.psum(jnp.sum(member_int * valid[:, None], 0).astype(jnp.float32), 'dp')  11.8 us
    all_gather x1, blocking collectives, per_device(): lax.all_gather(w_conv, 'dp', axis=2, tiled=True)  10.7 us
    all_gather x1, blocking collectives, per_device(): lax.all_gather(w_mid, 'dp', axis=1, tiled=True)  8.62 us
    unnamed x24, local copies, waits for them, and re-layouts  4.37 us
  transfers between devices with their start and end apart: 4, of which 1 were waited for; matrix products, arithmetic and copies ran while one was open for 11% of the time, Pallas kernels for 0%

commit v1 on v0

v1 whole, which is shorter than its diff:
```python
import functools

import jax
import jax.numpy as jnp
from jax import lax
from jax.experimental import pallas as pl
from jax.experimental.pallas import tpu as pltpu
from jax.sharding import PartitionSpec as P

MESH = pl.DeviceIdType.MESH
F32 = jnp.float32
BF16 = jnp.bfloat16
LANES = 128


def dot(a, b, ca, cb):
    return lax.dot_general(a, b, (((ca,), (cb,)), ((), ())), preferred_element_type=F32)


def gates(z):
    t = jnp.exp(-jnp.abs(z))
    inv = 1.0 / (1.0 + t)
    act = 0.2 * z + 0.8 * (jnp.maximum(z, 0.0) + jnp.log(1.0 + t))
    der = 0.2 + 0.8 * jnp.where(z >= 0.0, inv, t * inv)
    return act, der


def kernel(
    n, heads, scale_taps,
    feats, valid, owner, wc, wm, wo,
    out, gco, gmo, goo,
    xcat, wbuf, wall, obuf, h1s, d1s, e2s, ecat, dxs, hsum,
    hbuf, mbuf, gbuf, sbuf, rbuf, part, psend, precv, qsend, qrecv,
    lsem, wsend, wrecv, osend, orecv, hsend, hrecv, msend, mrecv,
    gsend, grecv, dsend, drecv, psems, qs, qr,
):
    local, length, width = feats.shape
    rows = wm.shape[0]
    slots = out.shape[0]
    half = n // 2
    me = lax.axis_index("dp")
    hd = lax.axis_index("head")
    chip, core = lax.div(me, 2), lax.rem(me, 2)
    partner = me + 1 - 2 * core

    def dp(j):
        return {"dp": j}

    def ring(i):
        return lax.rem(me + i, n)

    def peer(i):
        return 2 * lax.rem(chip + i, half) + core

    def remote(src, dst, s, r, device):
        return pltpu.make_async_remote_copy(
            src_ref=src, dst_ref=dst, send_sem=s, recv_sem=r, device_id=device, device_id_type=MESH
        )

    barrier = pltpu.get_barrier_semaphore()
    for i in range(1, n):
        pl.semaphore_signal(barrier, inc=1, device_id=dp(ring(i)), device_id_type=MESH)
    for i in range(1, heads):
        pl.semaphore_signal(
            barrier, inc=1, device_id={"head": lax.rem(hd + i, heads)}, device_id_type=MESH
        )
    own_conv = pltpu.make_async_copy(wc, wbuf.at[me, pl.ds(0, 3)], lsem.at[0])
    own_mid = pltpu.make_async_copy(wm, wbuf.at[me, 3], lsem.at[1])
    own_conv.start()
    own_mid.start()
    pick = (
        lax.broadcasted_iota(jnp.int32, (rows, width), 1)
        == me * rows + lax.broadcasted_iota(jnp.int32, (rows, width), 0)
    ).astype(F32)
    obuf[me] = dot(
        jnp.broadcast_to(wo[...], (8, rows)), pick.astype(BF16), 1, 0
    )
    row = lax.broadcasted_iota(jnp.int32, (length, width), 0)
    pl.semaphore_wait(barrier, n - 1 + heads - 1)

    firsts = []
    for i in range(1, half):
        firsts.append((
            remote(wc, wbuf.at[me, pl.ds(0, 3)], wsend.at[i, 0], wrecv.at[i, 0], dp(peer(i))),
            remote(wm, wbuf.at[me, 3], wsend.at[i, 1], wrecv.at[i, 1], dp(peer(i))),
        ))
    near = (
        remote(wc, wbuf.at[me, pl.ds(0, 3)], wsend.at[0, 0], wrecv.at[0, 0], dp(partner)),
        remote(wm, wbuf.at[me, 3], wsend.at[0, 1], wrecv.at[0, 1], dp(partner)),
    )
    outs = [
        remote(obuf.at[me], obuf.at[me], osend.at[i], orecv.at[i], dp(ring(i))) for i in range(1, n)
    ]
    for copies in firsts:
        for copy in copies:
            copy.start()
    for copy in near:
        copy.start()
    for copy in outs:
        copy.start()

    def prepare(k, _):
        x = jnp.where(row < valid[k], feats[k].astype(F32), 0.0)
        xcat[k, 0] = jnp.where(row == 0, 0.0, pltpu.roll(x, 1, 0)).astype(BF16)
        xcat[k, 1] = x.astype(BF16)
        xcat[k, 2] = jnp.where(row == length - 1, 0.0, pltpu.roll(x, length - 1, 0)).astype(BF16)
        return 0

    lax.fori_loop(0, local, prepare, 0)

    relays = []
    for i, copies in enumerate(firsts, 1):
        for copy in copies:
            copy.wait_recv()
        j = 2 * lax.rem(chip - i + half, half) + core
        relay = remote(wbuf.at[j], wbuf.at[j], wsend.at[i, 2], wrecv.at[i, 2], dp(partner))
        relay.start()
        relays.append(relay)
    own_conv.wait()
    own_mid.wait()
    for copy in near:
        copy.wait_recv()
    for copy in outs:
        copy.wait_recv()
    for relay in relays:
        relay.wait_recv()
    for j in range(n):
        for s in range(4):
            wall[s, j * rows:(j + 1) * rows, :] = wbuf[j, s]
    w_out = obuf[0]
    for j in range(1, n):
        w_out = w_out + obuf[j]
    w_out = w_out[0:1]

    def forward(k, _):
        x = [xcat[k, s] for s in range(3)]
        z1 = dot(x[0], wall[0], 1, 0) + dot(x[1], wall[1], 1, 0) + dot(x[2], wall[2], 1, 0)
        a1, d1 = gates(z1)
        h1 = a1.astype(BF16)
        h1s[k] = h1
        d1s[k] = d1
        z2 = dot(h1, wall[3], 1, 0)
        a2, d2 = gates(z2)
        live = row < valid[k]
        hsum[k] = jnp.sum(jnp.where(live, a2 + a1, 0.0), 0, keepdims=True)
        e2s[k] = jnp.where(live, w_out * d2, 0.0).astype(BF16)
        return 0

    lax.fori_loop(0, local, forward, 0)

    padded = hbuf.shape[1]
    line = lax.broadcasted_iota(jnp.int32, (padded, LANES), 0)
    lane = lax.broadcasted_iota(jnp.int32, (padded, LANES), 1)
    sums = jnp.zeros((padded, LANES), F32)
    owners = jnp.full((padded, LANES), -1.0, F32)
    counts = jnp.zeros((padded, LANES), F32)
    for k in range(local):
        total = jnp.sum(hsum[k] * w_out, 1, keepdims=True)
        sums = jnp.where(line == k, total, sums)
        owners = jnp.where(line == k, owner[k].astype(F32), owners)
        counts = jnp.where(line == k, valid[k].astype(F32), counts)
    hbuf[hd] = sums
    hcopies = [
        remote(
            hbuf.at[hd], hbuf.at[hd], hsend.at[i], hrecv.at[i], {"head": lax.rem(hd + i, heads)}
        )
        for i in range(1, heads)
    ]
    for copy in hcopies:
        copy.start()

    def middle(k, _):
        live = row < valid[k]
        back = dot(e2s[k], wall[3], 1, 1) + jnp.where(live, w_out, 0.0)
        e1 = back * d1s[k]
        ecat[k, 0] = jnp.where(row == length - 1, 0.0, pltpu.roll(e1, length - 1, 0)).astype(BF16)
        ecat[k, 1] = e1.astype(BF16)
        ecat[k, 2] = jnp.where(row == 0, 0.0, pltpu.roll(e1, 1, 0)).astype(BF16)
        return 0

    lax.fori_loop(0, local, middle, 0)
    for copy in hcopies:
        copy.wait_recv()
    all_taps = hbuf[0]
    for t in range(1, heads):
        all_taps = all_taps + hbuf[t]
    mbuf[me] = jnp.where(lane == 0, owners, jnp.where(lane == 1, counts, all_taps))
    mcopies = [
        remote(mbuf.at[me], mbuf.at[me], msend.at[i], mrecv.at[i], dp(ring(i))) for i in range(1, n)
    ]
    for copy in mcopies:
        copy.start()

    def inward(k, _):
        total = (
            dot(ecat[k, 0], wall[0], 1, 1)
            + dot(ecat[k, 1], wall[1], 1, 1)
            + dot(ecat[k, 2], wall[2], 1, 1)
        )
        dxs[k] = jnp.where(row < valid[k], total, 0.0)
        return 0

    lax.fori_loop(0, local, inward, 0)
    for copy in mcopies:
        copy.wait_recv()
    meta = mbuf[...]
    holder = meta[:, :, 0:1]
    device = lax.broadcasted_iota(jnp.int32, (n, padded, 1), 0)
    factors = []
    for k in range(local):
        mine = jnp.where(holder == owner[k].astype(F32), meta, 0.0)
        mine = jnp.sum(jnp.sum(mine, 0), 0, keepdims=True)
        norm = jnp.sqrt(scale_taps * mine[:, 1:2])
        strength = mine[:, 2:3] / norm
        t = jnp.exp(-jnp.abs(strength))
        gate = jnp.where(strength >= 0.0, t, 1.0) / (1.0 + t)
        factors.append(-float(length) * gate / norm)

    dcopies = []
    for i in list(range(1, n)) + [0]:
        dst = ring(i)
        block = None
        for k in range(local):
            here = jnp.where(owner[k] == dst, 1.0, 0.0).astype(F32)
            term = dxs[k] * (factors[k] * here)
            block = term if block is None else block + term
        if i == 0:
            rbuf[0] = block.astype(BF16)
        else:
            sbuf[i] = block.astype(BF16)
            copy = remote(sbuf.at[i], rbuf.at[i], dsend.at[i], drecv.at[i], dp(dst))
            copy.start()
            dcopies.append(copy)

    go = None
    for k in range(local):
        term = hsum[k] * factors[k]
        go = term if go is None else go + term
    gbuf[me] = jnp.broadcast_to(go, (8, width))
    gcopies = [
        remote(gbuf.at[me], gbuf.at[me], gsend.at[i], grecv.at[i], dp(ring(i))) for i in range(1, n)
    ]
    for copy in gcopies:
        copy.start()

    def flat(ref, s=None):
        pieces = [ref[k] if s is None else ref[k, s] for k in range(local)]
        return jnp.concatenate(pieces, 0)

    def scaled(ref, s=None):
        pieces = [
            ((ref[k] if s is None else ref[k, s]).astype(F32) * factors[k]).astype(BF16)
            for k in range(local)
        ]
        return jnp.concatenate(pieces, 0)

    x_all = flat(xcat, 1)
    for s in range(4):
        if s < 3:
            grad = dot(x_all, scaled(ecat, s), 0, 0)
        else:
            grad = dot(flat(h1s), scaled(e2s), 0, 0)
        for j in range(n):
            part[j, s] = grad[j * rows:(j + 1) * rows, :]
    for q in range(half):
        psend[q] = part[2 * q + 1 - core].astype(BF16)
    pcopy = remote(psend, precv, psems.at[0], psems.at[1], dp(partner))
    pcopy.start()
    pcopy.wait_recv()
    qcopies = []
    for i in range(1, half):
        q = lax.rem(chip + i, half)
        qsend[i] = (part[2 * q + core] + precv[q].astype(F32)).astype(BF16)
        copy = remote(qsend.at[i], qrecv.at[i], qs.at[i], qr.at[i], dp(2 * q + core))
        copy.start()
        qcopies.append(copy)
    blocks = float(n * local)
    grads = part[me] + precv[chip].astype(F32)

    owned = jnp.where(holder == me.astype(F32), 1.0, 0.0)

    def weights(i):
        j = lax.rem(me - i + n, n)
        has = jnp.sum(jnp.sum(jnp.where(device == j, owned, 0.0), 0), 0, keepdims=True)
        slot = jnp.sum(jnp.sum(jnp.where(device < j, owned, 0.0), 0), 0, keepdims=True)
        return [jnp.where(slot == float(c), has, 0.0).astype(BF16) for c in range(slots)]

    w = weights(0)
    for c in range(slots):
        out[c] = rbuf[0] * w[c]
    for i in range(1, n):
        dcopies[i - 1].wait_recv()
        w = weights(i)
        for c in range(slots):
            out[c] = out[c] + rbuf[i] * w[c]

    for copy in gcopies:
        copy.wait_recv()
    go = gbuf[0]
    for j in range(1, n):
        go = go + gbuf[j]
    go = pltpu.roll(go * (1.0 / blocks), lax.rem(width - me * rows, width), 1)
    goo[...] = go[0:1, :rows]
    for i in range(1, half):
        qcopies[i - 1].wait_recv()
        grads = grads + qrecv[i].astype(F32)
    grads = grads / blocks
    gco[...] = grads[0:3]
    gmo[...] = grads[3]

    for copies in firsts + [near]:
        for copy in copies:
            copy.wait_send()
    for copy in relays + outs + hcopies + mcopies + dcopies + gcopies + qcopies + [pcopy]:
        copy.wait_send()


def solution(mesh):
    n, heads = mesh.shape["dp"], mesh.shape["head"]

    def per_device(feats, valid, owner_map, w_conv, w_mid, w_out):
        local = owner_map.shape[0]
        width = feats.shape[2]
        length = feats.shape[1] // local
        rows = w_mid.shape[1]
        slots = n // 2
        half = n // 2
        padded = -(-local // 8) * 8
        dma = pltpu.SemaphoreType.DMA
        vmem = pl.BlockSpec(memory_space=pltpu.VMEM)
        smem = pl.BlockSpec(memory_space=pltpu.SMEM)
        block = (local, length, width)
        scratch = [
            pltpu.VMEM((local, 3, length, width), BF16),
            pltpu.VMEM((n, 4, rows, width), BF16),
            pltpu.VMEM((4, width, width), BF16),
            pltpu.VMEM((n, 8, width), F32),
            pltpu.VMEM(block, BF16),
            pltpu.VMEM(block, F32),
            pltpu.VMEM(block, BF16),
            pltpu.VMEM((local, 3, length, width), BF16),
            pltpu.VMEM(block, F32),
            pltpu.VMEM((local, 1, width), F32),
            pltpu.VMEM((heads, padded, LANES), F32),
            pltpu.VMEM((n, padded, LANES), F32),
            pltpu.VMEM((n, 8, width), F32),
            pltpu.VMEM((n, length, width), BF16),
            pltpu.VMEM((n, length, width), BF16),
            pltpu.VMEM((n, 4, rows, width), F32),
            pltpu.VMEM((half, 4, rows, width), BF16),
            pltpu.VMEM((half, 4, rows, width), BF16),
            pltpu.VMEM((half, 4, rows, width), BF16),
            pltpu.VMEM((half, 4, rows, width), BF16),
            dma((2,)), dma((half, 3)), dma((half, 3)), dma((n,)), dma((n,)),
            dma((heads,)), dma((heads,)), dma((n,)), dma((n,)),
            dma((n,)), dma((n,)), dma((n,)), dma((n,)),
            dma((2,)), dma((half,)), dma((half,)),
        ]
        returned, conv, mid, last = pl.pallas_call(
            functools.partial(kernel, n, heads, float(heads)),
            out_shape=(
                jax.ShapeDtypeStruct((slots, length, width), BF16),
                jax.ShapeDtypeStruct((3, rows, width), F32),
                jax.ShapeDtypeStruct((rows, width), F32),
                jax.ShapeDtypeStruct((1, rows), F32),
            ),
            in_specs=[vmem, smem, smem, vmem, vmem, vmem],
            out_specs=(vmem, vmem, vmem, vmem),
            scratch_shapes=scratch,
            compiler_params=pltpu.CompilerParams(
                collective_id=0, has_side_effects=True, vmem_limit_bytes=60 * 1024 * 1024
            ),
        )(
            feats.reshape(block), valid, owner_map, w_conv[0], w_mid[0], w_out
        )
        return (
            returned.reshape(1, slots * length, width), conv[None], mid[None], last
        )

    in_specs = (
        P("head", "dp", None), P("dp"), P("dp"),
        P("head", None, "dp", None), P("head", "dp", None), P("head", "dp"),
    )
    out_specs = (
        P("head", "dp", None), P("head", None, "dp", None), P("head", "dp", None), P("head", "dp"),
    )
    return jax.shard_map(
        per_device, mesh=mesh, in_specs=in_specs, out_specs=out_specs, check_vma=False
    )
```

time: 208 us -> 59.4 us (0.29)
  blocking collectives: 122 us -> 0 us
  Pallas kernels: 0 us -> 54.3 us
  waiting for transfers between devices: 29.7 us -> 0 us
  between operations: 16.3 us -> 0.65 us
  matrix products: 14.4 us -> 0 us
  other arithmetic: 9.45 us -> 0 us
  starting transfers between devices: 7.35 us -> 0 us
  local copies, waits for them, and re-layouts: 8.17 us -> 4.21 us
    pallas_call x0 -> x1, Pallas kernels: none -> 54.3 us  [per_device(): pl.pallas_call(functools.partial(kernel, n, heads, float(heads)), out_sha...]
    psum x2 -> x0, blocking collectives: 51.3 us -> none  [the longest x1 39.5 us: per_device(): lax.psum(jnp.dot(block_sums, members, precision=lax.Precision.HIGHEST), (...]
    unnamed x2 -> x0, blocking collectives: 37.1 us -> none
    reduce_scatter x2 -> x0, waiting for transfers between devices: 29.6 us -> none  [the longest x1 29.6 us: per_device(): lax.psum_scatter(grad_conv.astype(jnp.bfloat16), 'dp', scatter_dimension=...]
    all_gather x2 -> x0, blocking collectives: 19.4 us -> none  [the longest x1 10.7 us: per_device(): lax.all_gather(w_conv, 'dp', axis=2, tiled=True)]
    dot_general x19 -> x0, matrix products: 14.4 us -> none  [the longest x1 3.07 us: backward_pass(): jnp.dot(first_low.T, grad_mid_pre, preferred_element_type=jnp.float32)]
    squeeze x1 -> x0, blocking collectives: 14.3 us -> none  [per_device(): out_w = out_all[0]]
    all_to_all x2 -> x0, starting transfers between devices: 7.27 us -> none  [the longest x1 3.96 us: per_device(): lax.all_to_all(outgoing_grads, 'dp', split_axis=0, concat_axis=0, tiled=T...]
  transfers between devices with their start and end apart: 4 -> 0, of which waited for: 1 -> 0; matrix products, arithmetic and copies ran while one was open for 11% -> 0% of each run, Pallas kernels for 0% -> 0%
where the time goes in v1:
time: 59.4 us; the launch traced here: 59.2 us
  Pallas kernels  54.3 us (91%)
  local copies, waits for them, and re-layouts  4.21 us (7%)
  between operations  0.65 us (1%)
    pallas_call x1, Pallas kernels, per_device(): pl.pallas_call(functools.partial(kernel, n, heads, float(heads)), out_sha...  54.3 us
    unnamed x10, local copies, waits for them, and re-layouts  4.21 us

profile of v1, /device:TPU:0, one launch (start us, length us, event | category | flops | bytes accessed | tf_op | source)
XLA Modules:
  0.0 59.2 jit_solution(16861220231376633092)
XLA Ops:
  0.6 54.3 %shard_map.93 = (bf16[4,256,384]{2,1,0:T(8,128)(2,1)}, f32[3,48,384]{2,1,0:T(8,128)}, f32[48,384]{1,0:T(8,128)}, f32[1,48]{1,0:T(1,128)}) custom-call(bf16[2,256,384]{2,1,0:T(8,128)(2,1)} %bitcast.7, s32[2]{0:T(128)} %valid.1, s32[2]{0:T(128)} %owner.1, bf16[3,48,384]{2,1,0:T(8,128)(2,1)} %bitcast.9, bf16[48,384]{1,0:T(8,128)(2,1)} %bitcast.11, bf16[1,48]{1,0:T(2,128)(2,1)} %wo.1), custom_call_target="tpu_custom_call" | custom-call | tf_op jit(solution)/shard_map/pallas_call | solution.py:359
  54.9 0.0 copy-start
  55.0 2.1 %copy.14 = bf16[1,1024,384]{2,1,0:T(8,128)(2,1)} copy(bf16[1,1024,384]{2,1,0:T(8,128)(2,1)} %bitcast.6) | data formatting | bytes 1572864
  57.1 0.0 copy-done
  57.1 0.0 copy-start.1
  57.1 0.7 %copy.15 = f32[1,3,48,384]{3,2,1,0:T(8,128)} copy(f32[1,3,48,384]{3,2,1,0:T(8,128)S(1)} %bitcast.8) | data formatting | bytes 442368
  57.8 0.2 copy-done.1
  58.0 0.0 copy-start.2
  58.0 0.6 %copy.16 = f32[1,48,384]{2,1,0:T(8,128)} copy(f32[1,48,384]{2,1,0:T(8,128)S(1)} %bitcast.10) | data formatting | bytes 147456
  58.7 0.0 copy-done.2
  58.7 0.5 copy.17
Async XLA Ops:
  54.9 2.1 %copy-start = (f32[3,48,384]{2,1,0:T(8,128)S(1)}, f32[3,48,384]{2,1,0:T(8,128)}, u32[]{:S(2)}) copy-start(f32[3,48,384]{2,1,0:T(8,128)} %get-tuple-element.9) | copy-start | bytes 663556
  57.1 0.9 %copy-start.1 = (f32[48,384]{1,0:T(8,128)S(1)}, f32[48,384]{1,0:T(8,128)}, u32[]{:S(2)}) copy-start(f32[48,384]{1,0:T(8,128)} %get-tuple-element.10) | copy-start | bytes 221188
  58.0 0.6 %copy-start.2 = (f32[1,48]{1,0:T(1,128)S(1)}, f32[1,48]{1,0:T(1,128)}, u32[]{:S(2)}) copy-start(f32[1,48]{1,0:T(1,128)} %get-tuple-element.19) | copy-start | bytes 580

commit v2 on v1

--- a/solution.py
+++ b/solution.py
@@ -148,7 +148,7 @@
 
     lax.fori_loop(0, local, forward, 0)
 
-    padded = hbuf.shape[1]
+    padded = mbuf.shape[1]
     line = lax.broadcasted_iota(jnp.int32, (padded, LANES), 0)
     lane = lax.broadcasted_iota(jnp.int32, (padded, LANES), 1)
     sums = jnp.zeros((padded, LANES), F32)
@@ -159,14 +159,11 @@
         sums = jnp.where(line == k, total, sums)
         owners = jnp.where(line == k, owner[k].astype(F32), owners)
         counts = jnp.where(line == k, valid[k].astype(F32), counts)
-    hbuf[hd] = sums
-    hcopies = [
-        remote(
-            hbuf.at[hd], hbuf.at[hd], hsend.at[i], hrecv.at[i], {"head": lax.rem(hd + i, heads)}
-        )
-        for i in range(1, heads)
+    mbuf[me] = jnp.where(lane == 0, owners, jnp.where(lane == 1, counts, sums))
+    mcopies = [
+        remote(mbuf.at[me], mbuf.at[me], msend.at[i], mrecv.at[i], dp(ring(i))) for i in range(1, n)
     ]
-    for copy in hcopies:
+    for copy in mcopies:
         copy.start()
 
     def middle(k, _):
@@ -179,18 +176,6 @@
         return 0
 
     lax.fori_loop(0, local, middle, 0)
-    for copy in hcopies:
-        copy.wait_recv()
-    all_taps = hbuf[0]
-    for t in range(1, heads):
-        all_taps = all_taps + hbuf[t]
-    mbuf[me] = jnp.where(lane == 0, owners, jnp.where(lane == 1, counts, all_taps))
-    mcopies = [
-        remote(mbuf.at[me], mbuf.at[me], msend.at[i], mrecv.at[i], dp(ring(i))) for i in range(1, n)
-    ]
-    for copy in mcopies:
-        copy.start()
-
     def inward(k, _):
         total = (
             dot(ecat[k, 0], wall[0], 1, 1)
@@ -203,18 +188,15 @@
     lax.fori_loop(0, local, inward, 0)
     for copy in mcopies:
         copy.wait_recv()
-    meta = mbuf[...]
-    holder = meta[:, :, 0:1]
-    device = lax.broadcasted_iota(jnp.int32, (n, padded, 1), 0)
-    factors = []
-    for k in range(local):
-        mine = jnp.where(holder == owner[k].astype(F32), meta, 0.0)
-        mine = jnp.sum(jnp.sum(mine, 0), 0, keepdims=True)
-        norm = jnp.sqrt(scale_taps * mine[:, 1:2])
-        strength = mine[:, 2:3] / norm
-        t = jnp.exp(-jnp.abs(strength))
-        gate = jnp.where(strength >= 0.0, t, 1.0) / (1.0 + t)
-        factors.append(-float(length) * gate / norm)
+    hbuf[hd] = mbuf[...]
+    hcopies = [
+        remote(
+            hbuf.at[hd], hbuf.at[hd], hsend.at[i], hrecv.at[i], {"head": lax.rem(hd + i, heads)}
+        )
+        for i in range(1, heads)
+    ]
+    for copy in hcopies:
+        copy.start()
 
     dcopies = []
     for i in list(range(1, n)) + [0]:
@@ -222,7 +204,7 @@
         block = None
         for k in range(local):
             here = jnp.where(owner[k] == dst, 1.0, 0.0).astype(F32)
-            term = dxs[k] * (factors[k] * here)
+            term = dxs[k] * here
             block = term if block is None else block + term
         if i == 0:
             rbuf[0] = block.astype(BF16)
@@ -231,6 +213,27 @@
             copy = remote(sbuf.at[i], rbuf.at[i], dsend.at[i], drecv.at[i], dp(dst))
             copy.start()
             dcopies.append(copy)
+
+    for copy in hcopies:
+        copy.wait_recv()
+    meta = hbuf[0]
+    spread = lax.broadcasted_iota(jnp.int32, meta.shape, 2)
+    for t in range(1, heads):
+        meta = jnp.where(spread < 2, meta, meta + hbuf[t])
+    holder = meta[:, :, 0:1]
+    device = lax.broadcasted_iota(jnp.int32, (n, padded, 1), 0)
+
+    def factor_of(image):
+        mine = jnp.where(holder == image.astype(F32), meta, 0.0)
+        mine = jnp.sum(jnp.sum(mine, 0), 0, keepdims=True)
+        norm = jnp.sqrt(scale_taps * jnp.maximum(mine[:, 1:2], 1.0))
+        strength = mine[:, 2:3] / norm
+        t = jnp.exp(-jnp.abs(strength))
+        gate = jnp.where(strength >= 0.0, t, 1.0) / (1.0 + t)
+        return -float(length) * gate / norm
+
+    factors = [factor_of(owner[k]) for k in range(local)]
+    mine = factor_of(me)
 
     go = None
     for k in range(local):
@@ -283,16 +286,16 @@
         j = lax.rem(me - i + n, n)
         has = jnp.sum(jnp.sum(jnp.where(device == j, owned, 0.0), 0), 0, keepdims=True)
         slot = jnp.sum(jnp.sum(jnp.where(device < j, owned, 0.0), 0), 0, keepdims=True)
-        return [jnp.where(slot == float(c), has, 0.0).astype(BF16) for c in range(slots)]
+        return [jnp.where(slot == float(c), has * mine, 0.0) for c in range(slots)]
 
     w = weights(0)
     for c in range(slots):
-        out[c] = rbuf[0] * w[c]
+        out[c] = (rbuf[0].astype(F32) * w[c]).astype(BF16)
     for i in range(1, n):
         dcopies[i - 1].wait_recv()
         w = weights(i)
         for c in range(slots):
-            out[c] = out[c] + rbuf[i] * w[c]
+            out[c] = out[c] + (rbuf[i].astype(F32) * w[c]).astype(BF16)
 
     for copy in gcopies:
         copy.wait_recv()
@@ -341,7 +344,7 @@
             pltpu.VMEM((local, 3, length, width), BF16),
             pltpu.VMEM(block, F32),
             pltpu.VMEM((local, 1, width), F32),
-            pltpu.VMEM((heads, padded, LANES), F32),
+            pltpu.VMEM((heads, n, padded, LANES), F32),
             pltpu.VMEM((n, padded, LANES), F32),
             pltpu.VMEM((n, 8, width), F32),
             pltpu.VMEM((n, length, width), BF16),

time: 59.4 us -> 55.6 us (0.936)
  Pallas kernels: 54.3 us -> 50.5 us
    pallas_call x1, Pallas kernels: 54.3 us -> 50.5 us  [per_device(): pl.pallas_call(functools.partial(kernel, n, heads, float(heads)), out_sha...]
where the time goes in v2:
time: 55.6 us; the launch traced here: 55.4 us
  Pallas kernels  50.5 us (91%)
  local copies, waits for them, and re-layouts  4.21 us (8%)
  between operations  0.65 us (1%)
    pallas_call x1, Pallas kernels, per_device(): pl.pallas_call(functools.partial(kernel, n, heads, float(heads)), out_sha...  50.5 us
    unnamed x10, local copies, waits for them, and re-layouts  4.21 us

profile of v2, /device:TPU:0, one launch (start us, length us, event | category | flops | bytes accessed | tf_op | source)
XLA Modules:
  0.0 55.4 jit_solution(16848134085325299209)
XLA Ops:
  0.6 50.5 %shard_map.93 = (bf16[4,256,384]{2,1,0:T(8,128)(2,1)}, f32[3,48,384]{2,1,0:T(8,128)}, f32[48,384]{1,0:T(8,128)}, f32[1,48]{1,0:T(1,128)}) custom-call(bf16[2,256,384]{2,1,0:T(8,128)(2,1)} %bitcast.7, s32[2]{0:T(128)} %valid.1, s32[2]{0:T(128)} %owner.1, bf16[3,48,384]{2,1,0:T(8,128)(2,1)} %bitcast.9, bf16[48,384]{1,0:T(8,128)(2,1)} %bitcast.11, bf16[1,48]{1,0:T(2,128)(2,1)} %wo.1), custom_call_target="tpu_custom_call" | custom-call | tf_op jit(solution)/shard_map/pallas_call | solution.py:362
  51.1 0.0 copy-start
  51.1 2.1 %copy.14 = bf16[1,1024,384]{2,1,0:T(8,128)(2,1)} copy(bf16[1,1024,384]{2,1,0:T(8,128)(2,1)} %bitcast.6) | data formatting | bytes 1572864
  53.3 0.0 copy-done
  53.3 0.0 copy-start.1
  53.3 0.7 %copy.15 = f32[1,3,48,384]{3,2,1,0:T(8,128)} copy(f32[1,3,48,384]{3,2,1,0:T(8,128)S(1)} %bitcast.8) | data formatting | bytes 442368
  54.0 0.2 copy-done.1
  54.2 0.0 copy-start.2
  54.2 0.6 %copy.16 = f32[1,48,384]{2,1,0:T(8,128)} copy(f32[1,48,384]{2,1,0:T(8,128)S(1)} %bitcast.10) | data formatting | bytes 147456
  54.9 0.0 copy-done.2
  54.9 0.5 copy.17
Async XLA Ops:
  51.1 2.1 %copy-start = (f32[3,48,384]{2,1,0:T(8,128)S(1)}, f32[3,48,384]{2,1,0:T(8,128)}, u32[]{:S(2)}) copy-start(f32[3,48,384]{2,1,0:T(8,128)} %get-tuple-element.9) | copy-start | bytes 663556
  53.3 0.9 %copy-start.1 = (f32[48,384]{1,0:T(8,128)S(1)}, f32[48,384]{1,0:T(8,128)}, u32[]{:S(2)}) copy-start(f32[48,384]{1,0:T(8,128)} %get-tuple-element.10) | copy-start | bytes 221188
  54.2 0.6 %copy-start.2 = (f32[1,48]{1,0:T(1,128)S(1)}, f32[1,48]{1,0:T(1,128)}, u32[]{:S(2)}) copy-start(f32[1,48]{1,0:T(1,128)} %get-tuple-element.19) | copy-start | bytes 580
